TPU v7x, 256 devices: a whole 4x4x8 slice. The times are simulated.
256 devices in a mesh: section: 4 (over x), tok: 32 (over z, y), head: 2 (over core).
Axes of the slice: x: 4, y: 4, z: 8, core: 2. Of those that a mesh axis runs over, the one named last changes fastest.
Arguments:
- group_in: bfloat16 [4, 4096, 2048], P('section', 'tok'), may hold values from -6 to 6
- w_qkv: bfloat16 [4, 3, 2048, 2048], P('section', None, 'tok', 'head'), may hold values from -0.125 to 0.125
- w_out: bfloat16 [4, 2048, 2048], P('section', 'head', 'tok'), may hold values from -0.125 to 0.125
- step_sizes: float32 [4, 4096, 4], P('section', 'tok', 'head'), may hold values from 0.05 to 1
- fast_weights: bfloat16 [4, 4, 3, 512, 512], P('section', 'head'), may hold values from -0.25 to 0.25
- momentum: bfloat16 [4, 4, 3, 512, 512], P('section', 'head'), may hold values from -48 to 48
- momentum_decay: float32 [4, 4], P('section', 'head'), may hold values from 0.5 to 0.95
- fast_rate: float32 [4, 4], P('section', 'head'), may hold values from 0.3 to 1
Outputs:
- handed: bfloat16 [4, 4096, 2048], P('section', 'tok', 'head')
- fast_next: bfloat16 [4, 4, 3, 512, 512], P('section', 'head')
All inputs are finite; a program needn't handle non-finite values.
Results may differ from a plain program's by a relative error of at most 0.015.
Values may be sent and summed in bfloat16 or wider, within the bound.
No kernel may reach another device: no remote copies, remote signals or barrier semaphores. Data moves between devices by JAX's collectives and lax.ppermute only.
A program may use at most 128 MiB of HBM per device.

v0:
```python
import jax
import jax.numpy as jnp
from jax import lax
from jax.sharding import Mesh
from jax.sharding import PartitionSpec as P

NS_ITERS = 2
TOK = ("tok_0", "tok_1")
coef_linear = 3.4445
coef_cubic = -4.775
coef_quintic = 2.0315


def gathered_by_axis(shard, axes, dim):
    if not axes:
        return shard
    nearer = lax.all_gather(shard, axes[-1], axis=dim, tiled=True)
    return gathered_by_axis(nearer, axes[:-1], dim)


def split_up(shard, dim, count):
    lengths = shard.shape
    blocks = shard.reshape(*lengths[:dim], count, lengths[dim] // count, *lengths[dim + 1 :])
    return jnp.moveaxis(blocks, dim, 0)


def sum_at_owner(shard, axis, dim):
    count = lax.axis_size(axis)
    blocks = lax.all_to_all(split_up(shard, dim, count), axis, 0, 0, tiled=True)
    return jnp.sum(blocks.astype(jnp.float32), axis=0)


def passed_along(value, axis, steps):
    count = lax.axis_size(axis)
    pairs = [(source, (source + steps) % count) for source in range(count)]
    return lax.ppermute(value, axis, pairs)


def rms_rows(values_in, epsilon):
    return values_in * lax.rsqrt(jnp.mean(values_in * values_in, axis=-1, keepdims=True) + epsilon)


def fast_grads(key_rows, value_rows, step_rates, weights):
    gate_pre = jnp.einsum(
        "thi,hij->thj", key_rows, weights[:, 0], preferred_element_type=jnp.float32
    )
    up_pre = jnp.einsum("thi,hij->thj", key_rows, weights[:, 1], preferred_element_type=jnp.float32)
    squash = jax.nn.sigmoid(gate_pre)
    hidden = (gate_pre * squash * up_pre).astype(jnp.bfloat16)
    errors = (-(step_rates[:, :, None] * value_rows.astype(jnp.float32))).astype(jnp.bfloat16)
    back_hidden = jnp.einsum(
        "thi,hij->thj", errors, weights[:, 2], preferred_element_type=jnp.float32
    )
    grad_gate = (back_hidden * up_pre * squash * (1.0 + gate_pre * (1.0 - squash))).astype(
        jnp.bfloat16
    )
    grad_up = (back_hidden * gate_pre * squash).astype(jnp.bfloat16)
    grad_first = jnp.einsum("thi,thj->hij", key_rows, grad_gate, preferred_element_type=jnp.float32)
    grad_third = jnp.einsum("thi,thj->hij", key_rows, grad_up, preferred_element_type=jnp.float32)
    grad_second = jnp.einsum("thi,thj->hij", errors, hidden, preferred_element_type=jnp.float32)
    return jnp.stack([grad_first, grad_third, grad_second], axis=1)


def newton_step(rows_in, gathered):
    gram_matrix = jnp.einsum(
        "mij,mik->mjk", gathered, gathered, preferred_element_type=jnp.float32
    ).astype(jnp.bfloat16)
    cubic_term = jnp.einsum(
        "mij,mjk->mik", rows_in, gram_matrix, preferred_element_type=jnp.float32
    )
    quintic_term = jnp.einsum(
        "mij,mjk->mik",
        cubic_term.astype(jnp.bfloat16),
        gram_matrix,
        preferred_element_type=jnp.float32,
    )
    return (
        coef_linear * rows_in.astype(jnp.float32)
        + coef_cubic * cubic_term
        + coef_quintic * quintic_term
    ).astype(jnp.bfloat16)


def apply_fast(queries, updated):
    gate_pre = jnp.einsum(
        "thi,hij->thj", queries, updated[:, 0], preferred_element_type=jnp.float32
    )
    up_pre = jnp.einsum("thi,hij->thj", queries, updated[:, 1], preferred_element_type=jnp.float32)
    hidden = (jax.nn.silu(gate_pre) * up_pre).astype(jnp.bfloat16)
    output = jnp.einsum("thj,hij->thi", hidden, updated[:, 2], preferred_element_type=jnp.float32)
    return rms_rows(output, 1e-05).astype(jnp.bfloat16)


def shards(group_in, w_qkv, w_out, step_sizes, fast_weights, momentum, momentum_decay, fast_rate):
    tokens = group_in[0]
    tok_rows = tokens.shape[0]
    local_heads = fast_weights.shape[1]
    fan_width = fast_weights.shape[3]
    hid_width = fast_weights.shape[4]
    half_width = w_qkv.shape[3]
    projected = jnp.einsum(
        "td,jde->jte",
        tokens,
        lax.all_gather(w_qkv[0], TOK, axis=1, tiled=True),
        preferred_element_type=jnp.float32,
    )
    shaped = projected.reshape(3, tok_rows, local_heads, fan_width)
    queries = rms_rows(shaped[0], 1e-06).astype(jnp.bfloat16)
    key_rows = rms_rows(shaped[1], 1e-06).astype(jnp.bfloat16)
    value_rows = shaped[2].astype(jnp.bfloat16)
    gradients = fast_grads(key_rows, value_rows, step_sizes[0], fast_weights[0])
    decay_rate = momentum_decay[0][:, None, None, None]
    summed = lax.psum(gradients.astype(jnp.bfloat16), TOK).astype(jnp.float32)
    moment = decay_rate * momentum[0].astype(jnp.float32) + summed
    norm_values = jnp.sqrt(jnp.sum(moment * moment, axis=(2, 3), keepdims=True))
    iterate = (moment / (norm_values + 1e-06)).astype(jnp.bfloat16)
    iterate = iterate.reshape(local_heads * 3, fan_width, hid_width)
    for number in range(NS_ITERS):
        iterate = newton_step(iterate, iterate)
    iterate = iterate.reshape(local_heads, 3, fan_width, hid_width)
    updated = (
        fast_weights[0].astype(jnp.float32)
        - fast_rate[0][:, None, None, None] * iterate.astype(jnp.float32)
    ).astype(jnp.bfloat16)
    mixed_heads = apply_fast(queries, updated).reshape(tok_rows, half_width)
    partial_out = jnp.dot(
        mixed_heads, gathered_by_axis(w_out[0], TOK, 1), preferred_element_type=jnp.float32
    )
    summed_out = sum_at_owner(partial_out.astype(jnp.bfloat16), "head", 1)
    share_width = summed_out.shape[1]
    own_tokens = lax.dynamic_slice_in_dim(
        tokens, lax.axis_index("head") * share_width, share_width, 1
    )
    layer_out = (own_tokens.astype(jnp.float32) + summed_out).astype(jnp.bfloat16)
    handed = passed_along(layer_out[None], "section", 1)
    return (handed, updated[None])


def solution(mesh):
    torus = Mesh(
        mesh.devices.reshape(mesh.shape["section"], 8, 4, mesh.shape["head"]),
        ("section", "tok_0", "tok_1", "head"),
    )
    return jax.shard_map(
        shards,
        mesh=torus,
        in_specs=(
            P("section", TOK, None),
            P("section", None, TOK, "head"),
            P("section", "head", TOK),
            P("section", TOK, "head"),
            P("section", "head", None, None, None),
            P("section", "head", None, None, None),
            P("section", "head"),
            P("section", "head"),
        ),
        out_specs=(P("section", TOK, "head"), P("section", "head", None, None, None)),
        check_vma=False,
    )
```

profile of v0, /device:TPU:1, one launch (start us, length us, event | category | flops | bytes accessed | tf_op | source)
XLA Modules:
  0.0 375.4 jit_solution(4437180911537350289)
XLA Ops:
  8.0 0.0 all-gather.6.cloned.1.call-start
  8.0 0.7 all-gather.6.cloned.1.call-update
  8.7 0.0 all-reduce.2.cloned.1.call-start
  8.8 2.1 copy.71
  10.9 122.4 %all-gather.6.cloned.1.call-done = bf16[1,3,2048,1024]{3,2,1,0:T(8,128)(2,1)} async-done(((bf16[1,3,64,1024]{3,2,1,0:T(8,128)(2,1)}), bf16[1,3,2048,1024]{3,2,1,0:T(8,128)(2,1)}) %all-gather.6.cloned.1.call-update) | async-done | bytes 12582928 | tf_op jit(solution)/shard_map/all_gather | solution.py:104
  133.3 6.6 %fusion.19 = f32[3,128,1024]{1,2,0:T(8,128)S(1)} fusion(bf16[1,3,2048,1024]{3,2,1,0:T(8,128)(2,1)} %all-gather.6.cloned.1.call-done, bf16[1,128,2048]{2,1,0:T(8,128)(2,1)} %param.8), kind=kOutput, calls=%fused_computation.27 | convolution fusion | flops 1610612736 | bytes 14680064 | tf_op jit(solution)/shard_map/td,jde->jte/dot_general | solution.py:101
  139.9 0.9 fusion.46
  140.8 0.1 multiply_reduce_fusion.3
  140.9 0.3 convolution_bitcast_fusion.3
  141.3 0.3 convolution_bitcast_fusion.4
  141.6 0.0 copy-done.10
  141.7 0.3 convolution_bitcast_fusion.5
  142.0 0.5 fusion.23
  142.5 0.5 fusion.22
  143.0 0.5 fusion.24
  143.5 0.0 copy-start.6
  143.5 2.0 pad_maximum_fusion
  145.5 0.0 all-reduce.2.cloned.1.call-update
  145.6 0.0 all-gather.8.cloned.1.call-start
  145.6 0.0 copy-done.6
  145.6 10.9 %all-gather.1 = bf16[1,1024,256]{1,2,0:T(8,128)(2,1)} all-gather(bf16[1,1024,64]{1,2,0:T(8,128)(2,1)S(1)} %copy-done.6), channel_id=3, replica_groups=mesh['section'=4,'tok_0'=8,'tok_1'=4,'head'=2] {'tok_1'}, dimensions={2}, use_global_device_ids=true | all-gather | bytes 655360 | tf_op jit(solution)/shard_map/all_gather | solution.py:17
  156.6 0.0 all-gather.8.cloned.1.call-update
  156.6 1.1 multiply_reduce_fusion.2
  157.7 2.0 copy.44
  159.8 157.7 %all-reduce.2.cloned.1.call-done = bf16[2,3,512,512]{3,2,0,1:T(8,128)(2,1)} async-done(((bf16[2,3,512,512]{3,2,0,1:T(8,128)(2,1)}), bf16[2,3,512,512]{3,2,0,1:T(8,128)(2,1)}) %all-reduce.2.cloned.1.call-update) | async-done | bytes 3145744 | tf_op jit(solution)/shard_map/psum | solution.py:113
  317.5 0.0 copy-done.2
  317.5 0.0 copy-done.9
  317.5 3.5 multiply_reduce_fusion
  321.0 0.0 copy-done.3
  321.0 1.3 divide_convert_fusion
  322.3 0.2 copy.40
  322.5 1.8 convolution_convert_fusion.1
  324.3 1.8 fusion.47
  326.1 2.2 add_convert_fusion.1
  328.4 1.8 convolution_convert_fusion
  330.2 1.8 fusion.48
  332.0 0.0 copy-start.8
  332.0 2.5 fusion.7
  334.5 0.0 copy-start
  334.5 0.0 copy-done.8
  334.6 0.0 copy-start.5
  334.6 5.4 %fusion.4 = bf16[2,3,512,512]{3,2,0,1:T(8,128)(2,1)S(1)} fusion(f32[2,3,512,512]{3,2,1,0:T(8,128)S(1)} %bitcast.115, f32[2]{0:T(128)S(1)} %bitcast.131, bf16[1,2,3,512,512]{4,3,2,1,0:T(8,128)(2,1)} %param.12), kind=kLoop, calls=%fused_computation.6 | loop fusion | flops 6291456 | bytes 12582920 | tf_op jit(solution)/shard_map/convert_element_type | solution.py:124
  339.9 0.0 copy-done
  339.9 0.0 copy-start.4
  340.0 1.7 copy-done.4
  341.6 0.0 copy-done.5
  341.6 1.1 convolution_bitcast_fusion.1
  342.7 2.6 multiply_reduce_fusion.1
  345.3 0.1 multiply_convert_fusion
  345.4 0.0 all-gather.8.cloned.1.call-done
  345.4 0.0 copy-start.7
  345.4 0.0 slice-start.1
  345.5 3.9 %fusion.16 = bf16[128,2048]{1,0:T(8,128)(2,1)S(1)} fusion(bf16[128,1024]{0,1:T(8,128)(2,1)S(1)} %bitcast.130, bf16[1,1024,2048]{1,2,0:T(8,128)(2,1)} %all-gather.8.cloned.1.call-done), kind=kOutput, calls=%fused_computation.21 | convolution fusion | flops 537133056 | bytes 4980736 | tf_op jit(solution)/shard_map/dot_general | solution.py:126
  349.3 0.0 copy-start.1
  349.4 8.9 %all_to_all.5 = bf16[2,128,1024]{2,1,0:T(8,128)(2,1)S(1)} all-to-all(bf16[2,128,1024]{2,1,0:T(8,128)(2,1)S(1)} %bitcast.127), channel_id=1, replica_groups=mesh['section'=4,'tok_0'=8,'tok_1'=4,'head'=2] {'head'}, dimensions={0} | all-to-all | bytes 1048576 | tf_op jit(solution)/shard_map/all_to_all | solution.py:29
  358.3 0.1 convert_reduce_fusion
  358.4 0.0 copy-done.7
  358.4 0.1 fusion.29
  358.4 1.3 collective-permute-start
  359.7 0.0 slice-done
  359.7 0.0 slice-done.1
  359.7 2.8 subtract_convert_fusion
  362.5 4.7 %collective-permute-done = bf16[1,128,1024]{2,1,0:T(8,128)(2,1)S(1)} collective-permute-done((bf16[1,128,1024]{2,1,0:T(8,128)(2,1)S(1)}, bf16[1,128,1024]{2,1,0:T(8,128)(2,1)S(1)}, u32[]{:S(2)}, u32[]{:S(2)}) %collective-permute-start) | collective-permute-done | bytes 262176 | tf_op jit(solution)/shard_map/ppermute | solution.py:36
  367.2 0.7 copy.75
  (14 shorter events, 0.2 us)
Async XLA Ops:
  8.0 125.3 %all-gather.6.cloned.1.call-start = ((), (), s32[]{:S(2)}) async-start(), calls=%async_computation.2 | async-start | bytes 12976128 | tf_op jit(solution)/shard_map/all_gather | solution.py:104
  8.7 308.8 %all-reduce.2.cloned.1.call-start = ((), (), s32[]{:S(2)}) async-start(), calls=%async_computation.1 | async-start | bytes 6291456 | tf_op jit(solution)/shard_map/psum | solution.py:113
  140.8 0.9 copy-start.10
  143.5 2.1 copy-start.6
  145.5 172.0 %copy-start.2 = (bf16[1,2,3,512,512]{4,3,2,1,0:T(8,128)(2,1)S(1)}, bf16[1,2,3,512,512]{4,3,2,1,0:T(8,128)(2,1)}, u32[]{:S(2)}) copy-start(bf16[1,2,3,512,512]{4,3,2,1,0:T(8,128)(2,1)} %param.13) | copy-start | bytes 9437188
  145.5 172.0 %copy-start.9 = (f32[1,2]{1,0:T(1,128)S(1)}, f32[1,2]{1,0:T(1,128)}, u32[]{:S(2)}) copy-start(f32[1,2]{1,0:T(1,128)} %param.14) | copy-start | bytes 28
  145.6 199.9 %all-gather.8.cloned.1.call-start = ((), (), s32[]{:S(2)}) async-start(), calls=%async_computation.3 | async-start | bytes 4718592 | tf_op jit(solution)/shard_map/all_gather | solution.py:17
  317.5 3.5 copy-start.3
  332.0 2.5 copy-start.8
  334.5 5.4 %copy-start = (f32[6,512,512]{2,1,0:T(8,128)}, f32[6,512,512]{2,1,0:T(8,128)S(1)}, u32[]{:S(2)}) copy-start(f32[6,512,512]{2,1,0:T(8,128)S(1)} %fusion.7) | copy-start | bytes 18874372
  334.6 7.1 %copy-start.5 = (f32[128,2,512]{2,0,1:T(8,128)S(1)}, f32[128,2,512]{2,0,1:T(8,128)}, u32[]{:S(2)}) copy-start(f32[128,2,512]{2,0,1:T(8,128)} %copy.44) | copy-start | bytes 1572868
  339.9 1.7 copy-start.4
  342.7 17.0 %slice-start = ((s8[6291456]{0:T(1024)(128)(4,1)}), s8[2097152]{0:T(1024)(128)(4,1)S(1)}, s32[]{:S(2)}) async-start(s8[6291456]{0:T(1024)(128)(4,1)} %bitcast.116), calls=%async_computation.4 | async-start | bytes 4194304
  345.4 12.9 %copy-start.7 = (bf16[1,128,2048]{2,1,0:T(8,128)(2,1)S(1)}, bf16[1,128,2048]{2,1,0:T(8,128)(2,1)}, u32[]{:S(2)}) copy-start(bf16[1,128,2048]{2,1,0:T(8,128)(2,1)} %param.8) | copy-start | bytes 1572868
  345.4 14.3 %slice-start.1 = ((s8[6291456]{0:T(1024)(128)(4,1)}), s8[4194304]{0:T(1024)(128)(4,1)S(1)}, s32[]{:S(2)}) async-start(s8[6291456]{0:T(1024)(128)(4,1)} %bitcast.116), calls=%async_computation.5 | async-start | bytes 8388608
  349.3 10.4 %copy-start.1 = (bf16[1,2,3,512,512]{4,3,2,1,0:T(8,128)(2,1)S(1)}, bf16[1,2,3,512,512]{4,3,2,1,0:T(8,128)(2,1)}, u32[]{:S(2)}) copy-start(bf16[1,2,3,512,512]{4,3,2,1,0:T(8,128)(2,1)} %param.12) | copy-start | bytes 9437188
  358.4 8.8 %collective-permute-start = (bf16[1,128,1024]{2,1,0:T(8,128)(2,1)S(1)}, bf16[1,128,1024]{2,1,0:T(8,128)(2,1)S(1)}, u32[]{:S(2)}, u32[]{:S(2)}) collective-permute-start(bf16[1,128,1024]{2,1,0:T(8,128)(2,1)S(1)} %fusion.29), channel_id=1, source_target_pairs={{0,64},{64,128},{128,192},{192,0},{1,65},{65,129},{129,193},{193,1... | collective-permute-start | bytes 786440 | tf_op jit(solution)/shard_map/ppermute | solution.py:36
Sparse Core Ops, SparseCore 0:
  11.4 121.8 all-gather.5
  145.7 171.7 all-reduce.1
Sparse Core Ops, SparseCore 1:
  156.7 64.3 all-gather.7
where the time goes:
time: 376 us; the launch traced here: 375 us
  waiting for transfers between devices  286 us (76%)
  matrix products  28.7 us (8%)
  blocking collectives  19.8 us (5%)
  other arithmetic  16.4 us (4%)
  between operations  15.8 us (4%)
  local copies, waits for them, and re-layouts  7.67 us (2%)
    psum x1, waiting for transfers between devices, shards(): summed = lax.psum(gradients.astype(jnp.bfloat16), TOK).astype(jnp.float32)  158 us
    all_gather x1, waiting for transfers between devices, shards(): lax.all_gather(w_qkv[0], TOK, axis=1, tiled=True)  122 us
    all_gather x1, blocking collectives, gathered_by_axis(): nearer = lax.all_gather(shard, axes[-1], axis=dim, tiled=True)  10.9 us
    all_to_all x1, blocking collectives, sum_at_owner(): blocks = lax.all_to_all(split_up(shard, dim, count), axis, 0, 0, tiled=True)  8.89 us
    convert_element_type x2, other arithmetic, shards(): updated = (fast_weights[0].astype(jnp.float32) - fast_rate[0][:, None, No...  8.16 us
  transfers between devices with their start and end apart: 4, of which 3 were waited for; matrix products, arithmetic and copies ran while one was open for 9% of the time, Pallas kernels for 0%

commit v1 on v0

--- a/solution.py
+++ b/solution.py
@@ -101,7 +101,9 @@
     projected = jnp.einsum(
         "td,jde->jte",
         tokens,
-        lax.all_gather(w_qkv[0], TOK, axis=1, tiled=True),
+        jnp.concatenate(
+            lax.all_to_all(jnp.stack([w_qkv[0]] * lax.axis_size(TOK)), TOK, 0, 0), axis=1
+        ),
         preferred_element_type=jnp.float32,
     )
     shaped = projected.reshape(3, tok_rows, local_heads, fan_width)

time: 376 us -> 581 us (1.55)
  waiting for transfers between devices: 286 us -> 452 us
  blocking collectives: 19.8 us -> 35.1 us
  local copies, waits for them, and re-layouts: 7.67 us -> 22 us
  starting transfers between devices: 1.39 us -> 13.8 us
    all_to_all x0 -> x1, waiting for transfers between devices: none -> 285 us  [shards(): lax.all_to_all(jnp.stack([w_qkv[0]] * lax.axis_size(TOK)), TOK, 0, 0)]
    all_gather x1 -> x0, waiting for transfers between devices: 122 us -> none  [shards(): lax.all_gather(w_qkv[0], TOK, axis=1, tiled=True)]
    all_gather x1, blocking collectives: 10.9 us -> 26.2 us  [gathered_by_axis(): nearer = lax.all_gather(shard, axes[-1], axis=dim, tiled=True)]
    all_to_all x0 -> x1, starting transfers between devices: none -> 12.4 us  [shards(): lax.all_to_all(jnp.stack([w_qkv[0]] * lax.axis_size(TOK)), TOK, 0, 0)]
    another operation x0 -> x1, local copies, waits for them, and re-layouts: none -> 7.08 us  [shards(): jnp.stack([w_qkv[0]] * lax.axis_size(TOK))]
    all_to_all x0 -> x1, local copies, waits for them, and re-layouts: none -> 6.42 us  [shards(): lax.all_to_all(jnp.stack([w_qkv[0]] * lax.axis_size(TOK)), TOK, 0, 0)]
  transfers between devices with their start and end apart: 4 -> 4, of which waited for: 3 -> 3; matrix products, arithmetic and copies ran while one was open for 9% -> 6% of each run, Pallas kernels for 0% -> 0%
where the time goes in v1:
time: 581 us; the launch traced here: 580 us
  waiting for transfers between devices  452 us (78%)
  blocking collectives  35.1 us (6%)
  matrix products  25.5 us (4%)
  local copies, waits for them, and re-layouts  22 us (4%)
  other arithmetic  16.4 us (3%)
  between operations  15.8 us (3%)
  starting transfers between devices  13.8 us (2%)
    all_to_all x1, waiting for transfers between devices, shards(): lax.all_to_all(jnp.stack([w_qkv[0]] * lax.axis_size(TOK)), TOK, 0, 0)  285 us
    psum x1, waiting for transfers between devices, shards(): summed = lax.psum(gradients.astype(jnp.bfloat16), TOK).astype(jnp.float32)  162 us
    all_gather x1, blocking collectives, gathered_by_axis(): nearer = lax.all_gather(shard, axes[-1], axis=dim, tiled=True)  26.2 us
    all_to_all x1, starting transfers between devices, shards(): lax.all_to_all(jnp.stack([w_qkv[0]] * lax.axis_size(TOK)), TOK, 0, 0)  12.4 us
  transfers between devices with their start and end apart: 4, of which 3 were waited for; matrix products, arithmetic and copies ran while one was open for 6% of the time, Pallas kernels for 0%

profile of v1, /device:TPU:1, one launch (start us, length us, event | category | flops | bytes accessed | tf_op | source)
XLA Modules:
  0.0 580.4 jit_solution(15801742802956196037)
XLA Ops:
  8.0 7.1 %stack.19 = bf16[32,3,64,1024]{3,2,1,0:T(8,128)(2,1)} broadcast(bf16[3,64,1024]{2,1,0:T(8,128)(2,1)} %bitcast.131), dimensions={1,2,3} | broadcast | bytes 12976128 | tf_op jit(solution)/shard_map/stack | solution.py:105
  15.1 12.4 %all-to-all-start = ((bf16[32,3,64,1024]{3,2,1,0:T(8,128)(2,1)}), bf16[32,3,64,1024]{3,2,1,0:T(8,128)(2,1)}, u32[]{:S(2)}, u32[]{:S(2)}) async-start(bf16[32,3,64,1024]{3,2,1,0:T(8,128)(2,1)} %stack.19), calls=%async_computation | async-start | bytes 25165824 | tf_op jit(solution)/shard_map/all_to_all | solution.py:105
  27.5 0.0 all-reduce.2.cloned.1.call-start
  27.5 0.0 copy-done.1
  27.5 1.9 copy.73
  29.4 285.1 %all-to-all-done = bf16[32,3,64,1024]{3,2,1,0:T(8,128)(2,1)} async-done(((bf16[32,3,64,1024]{3,2,1,0:T(8,128)(2,1)}), bf16[32,3,64,1024]{3,2,1,0:T(8,128)(2,1)}, u32[]{:S(2)}, u32[]{:S(2)}) %all-to-all-start) | async-done | bytes 12582944 | tf_op jit(solution)/shard_map/all_to_all | solution.py:105
  314.5 6.4 %copy.36 = bf16[32,3,64,1024]{3,2,0,1:T(8,128)(2,1)S(1)} copy(bf16[32,3,64,1024]{3,2,1,0:T(8,128)(2,1)} %all-to-all-done) | data formatting | bytes 25165824 | tf_op jit(solution)/shard_map/all_to_all | solution.py:105
  321.0 0.0 copy-done.9
  321.0 3.5 convolution_bitcast_fusion
  324.5 0.0 copy-start.3
  324.5 0.9 fusion.41
  325.4 0.1 multiply_reduce_fusion.3
  325.5 1.0 copy-done.3
  326.6 0.3 convolution_bitcast_fusion.4
  326.9 0.3 convolution_bitcast_fusion.5
  327.3 0.0 copy-done.13
  327.3 0.3 convolution_bitcast_fusion.6
  327.6 0.5 fusion.18
  328.1 0.5 fusion.17
  328.7 0.5 fusion.19
  329.1 0.0 copy-start.8
  329.2 2.0 pad_maximum_fusion
  331.2 0.0 all-reduce.2.cloned.1.call-update
  331.2 0.0 all-gather.4.cloned.1.call-start
  331.2 0.0 copy-done.8
  331.3 26.2 %all-gather = bf16[1,1024,256]{1,2,0:T(8,128)(2,1)} all-gather(bf16[1,1024,64]{1,2,0:T(8,128)(2,1)S(1)} %copy-done.8), channel_id=2, replica_groups=mesh['section'=4,'tok_0'=8,'tok_1'=4,'head'=2] {'tok_1'}, dimensions={2}, use_global_device_ids=true | all-gather | bytes 655360 | tf_op jit(solution)/shard_map/all_gather | solution.py:17
  357.4 0.0 all-gather.4.cloned.1.call-update
  357.5 1.1 multiply_reduce_fusion.2
  358.6 2.1 copy.45
  360.7 161.9 %all-reduce.2.cloned.1.call-done = bf16[2,3,512,512]{3,2,0,1:T(8,128)(2,1)} async-done(((bf16[2,3,512,512]{3,2,0,1:T(8,128)(2,1)}), bf16[2,3,512,512]{3,2,0,1:T(8,128)(2,1)}) %all-reduce.2.cloned.1.call-update) | async-done | bytes 3145744 | tf_op jit(solution)/shard_map/psum | solution.py:115
  522.6 3.5 multiply_reduce_fusion
  526.0 1.3 divide_convert_fusion
  527.3 0.2 copy.41
  527.6 1.8 convolution_convert_fusion.1
  529.4 1.8 fusion.42
  531.2 2.2 add_convert_fusion.1
  533.4 1.8 convolution_convert_fusion
  535.3 1.8 fusion.43
  537.1 0.0 copy-start.11
  537.1 2.5 fusion.5
  539.6 0.0 copy-start
  539.6 0.0 copy-done.11
  539.6 0.0 copy-start.7
  539.6 5.4 fusion.2
  545.0 0.0 copy-start.6
  545.0 1.7 copy-done.6
  546.7 1.1 convolution_bitcast_fusion.2
  547.8 2.6 multiply_reduce_fusion.1
  550.4 0.1 multiply_convert_fusion
  550.5 0.0 all-gather.4.cloned.1.call-done
  550.5 0.0 copy-start.10
  550.5 0.0 slice-start.1
  550.5 3.8 fusion.14
  554.4 0.0 copy-start.2
  554.4 8.9 %all_to_all.10 = bf16[2,128,1024]{2,1,0:T(8,128)(2,1)S(1)} all-to-all(bf16[2,128,1024]{2,1,0:T(8,128)(2,1)S(1)} %bitcast.127), channel_id=1, replica_groups=mesh['section'=4,'tok_0'=8,'tok_1'=4,'head'=2] {'head'}, dimensions={0} | all-to-all | bytes 1048576 | tf_op jit(solution)/shard_map/all_to_all | solution.py:29
  563.3 0.1 convert_reduce_fusion
  563.4 0.0 copy-done.10
  563.4 0.1 fusion.24
  563.5 1.3 collective-permute-start
  564.8 0.0 slice-done
  564.8 0.0 copy-done.2
  564.8 2.8 subtract_convert_fusion
  567.6 4.7 collective-permute-done
  572.3 0.7 copy.77
  (21 shorter events, 0.2 us)
Async XLA Ops:
  15.1 12.5 %copy-start.1 = (bf16[1,2,3,512,512]{4,3,2,1,0:T(8,128)(2,1)S(1)}, bf16[1,2,3,512,512]{4,3,2,1,0:T(8,128)(2,1)}, u32[]{:S(2)}) copy-start(bf16[1,2,3,512,512]{4,3,2,1,0:T(8,128)(2,1)} %param.12) | copy-start | bytes 9437188
  15.1 299.5 %all-to-all-start = ((bf16[32,3,64,1024]{3,2,1,0:T(8,128)(2,1)}), bf16[32,3,64,1024]{3,2,1,0:T(8,128)(2,1)}, u32[]{:S(2)}, u32[]{:S(2)}) async-start(bf16[32,3,64,1024]{3,2,1,0:T(8,128)(2,1)} %stack.19), calls=%async_computation | async-start | bytes 25165824 | tf_op jit(solution)/shard_map/all_to_all | solution.py:105
  27.5 495.1 %all-reduce.2.cloned.1.call-start = ((), (), s32[]{:S(2)}) async-start(), calls=%async_computation.2 | async-start | bytes 6291456 | tf_op jit(solution)/shard_map/psum | solution.py:115
  29.4 291.6 %copy-start.9 = (bf16[1,128,2048]{2,1,0:T(8,128)(2,1)S(1)}, bf16[1,128,2048]{2,1,0:T(8,128)(2,1)}, u32[]{:S(2)}) copy-start(bf16[1,128,2048]{2,1,0:T(8,128)(2,1)} %param.8) | copy-start | bytes 1572868
  324.5 2.1 copy-start.3
  325.4 1.9 copy-start.13
  329.1 2.1 copy-start.8
  331.2 191.4 %copy-start.4 = (bf16[1,2,3,512,512]{4,3,2,1,0:T(8,128)(2,1)S(1)}, bf16[1,2,3,512,512]{4,3,2,1,0:T(8,128)(2,1)}, u32[]{:S(2)}) copy-start(bf16[1,2,3,512,512]{4,3,2,1,0:T(8,128)(2,1)} %param.13) | copy-start | bytes 9437188
  331.2 191.4 %copy-start.12 = (f32[1,2]{1,0:T(1,128)S(1)}, f32[1,2]{1,0:T(1,128)}, u32[]{:S(2)}) copy-start(f32[1,2]{1,0:T(1,128)} %param.14) | copy-start | bytes 28
  331.2 219.3 %all-gather.4.cloned.1.call-start = ((), (), s32[]{:S(2)}) async-start(), calls=%async_computation.3 | async-start | bytes 4718592 | tf_op jit(solution)/shard_map/all_gather | solution.py:17
  522.6 3.5 copy-start.5
  537.1 2.5 copy-start.11
  539.6 5.4 copy-start
  539.6 7.1 %copy-start.7 = (f32[128,2,512]{2,0,1:T(8,128)S(1)}, f32[128,2,512]{2,0,1:T(8,128)}, u32[]{:S(2)}) copy-start(f32[128,2,512]{2,0,1:T(8,128)} %copy.45) | copy-start | bytes 1572868
  545.0 1.7 copy-start.6
  547.8 17.0 %slice-start = ((s8[6291456]{0:T(1024)(128)(4,1)}), s8[2097152]{0:T(1024)(128)(4,1)S(1)}, s32[]{:S(2)}) async-start(s8[6291456]{0:T(1024)(128)(4,1)} %bitcast.115), calls=%async_computation.4 | async-start | bytes 4194304
  550.5 12.9 %copy-start.10 = (bf16[1,128,2048]{2,1,0:T(8,128)(2,1)S(1)}, bf16[1,128,2048]{2,1,0:T(8,128)(2,1)}, u32[]{:S(2)}) copy-start(bf16[1,128,2048]{2,1,0:T(8,128)(2,1)} %param.8) | copy-start | bytes 1572868
  550.5 14.3 %slice-start.1 = ((s8[6291456]{0:T(1024)(128)(4,1)}), s8[4194304]{0:T(1024)(128)(4,1)S(1)}, s32[]{:S(2)}) async-start(s8[6291456]{0:T(1024)(128)(4,1)} %bitcast.115), calls=%async_computation.5 | async-start | bytes 8388608
  554.4 10.4 %copy-start.2 = (bf16[1,2,3,512,512]{4,3,2,1,0:T(8,128)(2,1)S(1)}, bf16[1,2,3,512,512]{4,3,2,1,0:T(8,128)(2,1)}, u32[]{:S(2)}) copy-start(bf16[1,2,3,512,512]{4,3,2,1,0:T(8,128)(2,1)} %param.12) | copy-start | bytes 9437188
  563.5 8.8 %collective-permute-start = (bf16[1,128,1024]{2,1,0:T(8,128)(2,1)S(1)}, bf16[1,128,1024]{2,1,0:T(8,128)(2,1)S(1)}, u32[]{:S(2)}, u32[]{:S(2)}) collective-permute-start(bf16[1,128,1024]{2,1,0:T(8,128)(2,1)S(1)} %fusion.24), channel_id=1, source_target_pairs={{0,64},{64,128},{128,192},{192,0},{1,65},{65,129},{129,193},{193,1... | collective-permute-start | bytes 786440 | tf_op jit(solution)/shard_map/ppermute | solution.py:36
Sparse Core Ops, SparseCore 0:
  331.3 191.1 all-reduce.1
Sparse Core Ops, SparseCore 1:
  357.6 68.1 all-gather.3
